TPU v7x, 512 devices: a whole 4x4x16 slice. The times are simulated.
512 devices in a mesh: cfd: 64 (over z_lo, x, core), ac: 8 (over y, z_hi).
Axes of the slice: x: 4, y: 4, z: 16 (z_hi: 2, z_lo: 8; z = z_hi * 8 + z_lo), core: 2. Of those that a mesh axis runs over, the one named last changes fastest.
Arguments:
- surface_raw: bfloat16 [5, 65536, 1024], P(None, ('cfd', 'ac')), may hold values from -6 to 6
- area_normals: bfloat16 [3, 65536], P(None, ('cfd', 'ac')), may hold values from -6 to 6
- kernel_weights: bfloat16 [2, 3, 2048, 65536], P(None, None, None, ('cfd', 'ac')), may hold values from -0.0390625 to 0.0390625
- block_map: int32 [8, 64, 64], P('ac', 'cfd'), may hold values from 0 to 63, as said below
- band_observers: int32 [16, 128], replicated, may hold values from 0 to 2047, as said below
- band_lags: int32 [16], replicated, may hold values from 0 to 511
Outputs:
- acoustic: float32 [2048, 512], P('cfd', 'ac')
Inputs may be any that keep to these rules, and one draw needn't show every extreme that they name: block_map[j, s, :] is a permutation of 0 to 63 for every j and s. `band_observers`: every observer appears exactly once.
All inputs are finite; a program needn't handle non-finite values.
Results may differ from a plain program's by a relative error of at most 0.0042.
Values may be sent and summed in bfloat16 or wider, within the bound.
A program may use at most 64 MiB of HBM per device.

v0:
```python
import jax
import jax.numpy as jnp
from jax import lax
from jax.sharding import PartitionSpec as P


def cut_along(array, dim, count):
    lengths = array.shape
    tiles = array.reshape(*lengths[:dim], count, lengths[dim] // count, *lengths[dim + 1 :])
    return jnp.moveaxis(tiles, dim, 0)


def summed_on_arrival(array, axis, dim):
    count = lax.axis_size(axis)
    tiles = lax.all_to_all(cut_along(array, dim, count), axis, 0, 0, tiled=True)
    return jnp.sum(tiles.astype(jnp.float32), axis=0)


def sum_at_owner(array, axis, dim):
    count = lax.axis_size(axis)
    tiles = lax.all_to_all(cut_along(array, dim, count), axis, 0, 0, tiled=True)
    return jnp.sum(tiles, axis=0)


def thickness(surface, normals):
    along = surface[2].astype(jnp.float32) * normals[0].astype(jnp.float32)[:, None]
    along = along + surface[3].astype(jnp.float32) * normals[1].astype(jnp.float32)[:, None]
    along = along + surface[4].astype(jnp.float32) * normals[2].astype(jnp.float32)[:, None]
    return (surface[1].astype(jnp.float32) * along).astype(jnp.bfloat16)


def rates(series):
    step = series[:, 1:].astype(jnp.float32) - series[:, :-1].astype(jnp.float32)
    first = jnp.zeros((series.shape[0], 1), jnp.float32)
    return jnp.concatenate([first, step], axis=1).astype(jnp.bfloat16)


def reorder_blocks(array, block_order, blocks):
    lead = array.shape[0]
    rest = array.shape[2:]
    grouped = array.reshape((lead, blocks, -1))
    picked = jnp.take(grouped, block_order, axis=1)
    return picked.reshape((lead, array.shape[1]) + rest)


def local(surface_raw, area_normals, kernel_weights, block_map, band_observers, band_lags):
    blocks = lax.axis_size("cfd")
    block_order = block_map[0, 0]
    thick = thickness(surface_raw, area_normals)
    outgoing = reorder_blocks(jnp.stack([thick, surface_raw[0]]), block_order, blocks)
    arrived = lax.all_to_all(outgoing, "cfd", split_axis=1, concat_axis=1, tiled=True)
    thickness_in = arrived[0]
    pressure_in = arrived[1]
    sources = jnp.stack([rates(thickness_in), rates(pressure_in), pressure_in])
    out_len = sources.shape[2] // 2
    tap_count = kernel_weights.shape[0]
    band_count = band_observers.shape[0]
    band_width = band_observers.shape[1]
    observer_count = kernel_weights.shape[2]

    def one_band(carry, band_index):
        delay = band_lags[band_index]
        start = band_index * band_width
        chosen = lax.dynamic_slice_in_dim(kernel_weights, start, band_width, 2)
        windows = jnp.stack(
            [
                lax.dynamic_slice_in_dim(sources, out_len - delay - shift_step, out_len, 2)
                for shift_step in range(tap_count)
            ]
        )
        contribution = jnp.einsum(
            "kcof,kcft->ot", chosen, windows, preferred_element_type=jnp.float32
        )
        return (carry, contribution)

    _, banded = lax.scan(one_band, 0, jnp.arange(band_count, dtype=jnp.int32))
    banded = banded.reshape(observer_count, out_len)
    flat_ids = band_observers.reshape(-1)
    inverse = (
        jnp.zeros((observer_count,), jnp.int32)
        .at[flat_ids]
        .set(jnp.arange(observer_count, dtype=jnp.int32))
    )
    partial_value = jnp.take(banded, inverse, axis=0)
    reduced = summed_on_arrival(partial_value.astype(jnp.bfloat16), "cfd", 0)
    result = sum_at_owner(reduced, "ac", 1)
    return result


def solution(mesh):
    placed = (
        P(None, ("cfd", "ac"), None),
        P(None, ("cfd", "ac")),
        P(None, None, None, ("cfd", "ac")),
        P("ac", "cfd", None),
        P(),
        P(),
    )
    return jax.shard_map(
        local, mesh=mesh, in_specs=placed, out_specs=P("cfd", "ac"), check_vma=False
    )
```

profile of v0, /device:TPU:1, one launch (start us, length us, event | category | flops | bytes accessed | tf_op | source)
XLA Modules:
  0.0 332.7 jit_solution(5581146758800844564)
XLA Ops:
  0.0 0.7 fusion.9
  0.7 0.7 compare_and_fusion.1
  1.4 0.8 bitcast_convert_fusion.2
  2.2 1.5 multiply_convert_fusion
  4.1 1.2 pad_maximum_fusion.1
  5.3 1.6 gather_fusion
  7.7 1.3 copy.23
  9.0 17.0 %all-to-all-start = ((bf16[2,128,1024]{2,0,1:T(2,128)(2,1)}), bf16[2,128,1024]{2,0,1:T(2,128)(2,1)S(1)}, u32[]{:S(2)}, u32[]{:S(2)}) async-start(bf16[2,128,1024]{2,0,1:T(2,128)(2,1)} %copy.23), calls=%async_computation | async-start | bytes 1048576 | tf_op jit(solution)/shard_map/all_to_all | solution.py:51
  26.1 8.0 %scatter_custom_fusion = s32[2048]{0:T(1024)S(1)} fusion(s32[2048]{0:T(1024)S(1)} %bitcast.69, s32[2048]{0:T(1024)S(1)} %iota.6, s32[]{:T(128)} %constant.111.clone.1), kind=kCustom, calls=%fused_computation.29 | custom fusion | bytes 8196 | tf_op jit(solution)/shard_map/scatter | solution.py:82
  34.2 21.9 %all-to-all-done = bf16[2,128,1024]{2,0,1:T(2,128)(2,1)S(1)} async-done(((bf16[2,128,1024]{2,0,1:T(2,128)(2,1)}), bf16[2,128,1024]{2,0,1:T(2,128)(2,1)S(1)}, u32[]{:S(2)}, u32[]{:S(2)}) %all-to-all-start) | async-done | bytes 524320 | tf_op jit(solution)/shard_map/all_to_all | solution.py:51
  56.2 0.7 fusion.10
  57.9 135.5 %while.14 = (s32[]{:T(128)}, bf16[16,128,512]{2,1,0:T(8,128)(2,1)S(1)}, s32[16]{0:T(128)S(1)}, bf16[2,3,2048,128]{3,2,1,0:T(8,128)(2,1)}, s32[16]{0:T(128)S(1)},...) while((s32[]{:T(128)}, ...), condition=%wide.region_2.3_spmd, body=%wide.region_1.2_spmd.sunk | while | flops 101056528 | bytes 2818909 | solution.py:76
  57.9 0.6 dynamic_slice.57
  63.2 1.1 dynamic-slice_bitcast_fusion.3
  65.0 1.4 fusion.16
  66.4 0.6 dynamic_slice.57
  71.7 1.1 dynamic-slice_bitcast_fusion.3
  73.5 1.4 fusion.16
  74.9 0.6 dynamic_slice.57
  80.2 1.1 dynamic-slice_bitcast_fusion.3
  81.9 1.4 fusion.16
  83.4 0.6 dynamic_slice.57
  88.7 1.1 dynamic-slice_bitcast_fusion.3
  90.4 1.4 fusion.16
  91.8 0.6 dynamic_slice.57
  97.1 1.1 dynamic-slice_bitcast_fusion.3
  98.9 1.4 fusion.16
  100.3 0.6 dynamic_slice.57
  105.6 1.1 dynamic-slice_bitcast_fusion.3
  107.3 1.4 fusion.16
  108.8 0.6 dynamic_slice.57
  114.1 1.1 dynamic-slice_bitcast_fusion.3
  115.8 1.4 fusion.16
  117.2 0.6 dynamic_slice.57
  122.5 1.1 dynamic-slice_bitcast_fusion.3
  124.3 1.4 fusion.16
  125.7 0.6 dynamic_slice.57
  131.0 1.1 dynamic-slice_bitcast_fusion.3
  132.8 1.4 fusion.16
  134.2 0.6 dynamic_slice.57
  139.5 1.1 dynamic-slice_bitcast_fusion.3
  141.2 1.4 fusion.16
  142.6 0.6 dynamic_slice.57
  147.9 1.1 dynamic-slice_bitcast_fusion.3
  149.7 1.4 fusion.16
  151.1 0.6 dynamic_slice.57
  156.4 1.1 dynamic-slice_bitcast_fusion.3
  158.2 1.4 fusion.16
  159.6 0.6 dynamic_slice.57
  164.9 1.1 dynamic-slice_bitcast_fusion.3
  166.6 1.4 fusion.16
  168.0 0.6 dynamic_slice.57
  173.3 1.1 dynamic-slice_bitcast_fusion.3
  175.1 1.4 fusion.16
  181.8 1.1 dynamic-slice_bitcast_fusion.3
  183.6 1.4 fusion.16
  190.3 1.1 dynamic-slice_bitcast_fusion.3
  192.0 1.4 fusion.16
  193.4 9.2 %gather_fusion.1 = bf16[2048,512]{1,0:T(8,128)(2,1)} fusion(bf16[2048,512]{1,0:T(8,128)(2,1)S(1)} %bitcast.62, s32[2048]{0:T(1024)S(1)} %fusion.6), kind=kCustom, calls=%fused_computation.1 | custom fusion | bytes 4202496 | tf_op jit(solution)/shard_map/jit(_take)/gather | solution.py:84
  202.6 1.9 select_convert_fusion
  204.6 101.9 %all_to_all.15 = bf16[64,32,512]{2,1,0:T(8,128)(2,1)S(1)} all-to-all(bf16[64,32,512]{2,1,0:T(8,128)(2,1)S(1)} %select_convert_fusion), channel_id=1, replica_groups=mesh['cfd'=64,'ac'=8] {'cfd'}, dimensions={0} | all-to-all | bytes 4194304 | tf_op jit(solution)/shard_map/all_to_all | solution.py:15
  307.0 23.6 %all_to_all.16 = f32[8,1,2048]{2,1,0:T(1,128)S(1)} all-to-all(f32[8,1,2048]{2,1,0:T(1,128)S(1)} %reshape.173), channel_id=1, replica_groups=mesh['cfd'=64,'ac'=8] {'ac'}, dimensions={0} | all-to-all | bytes 131072 | tf_op jit(solution)/shard_map/all_to_all | solution.py:21
  331.2 0.8 reduce
  332.1 0.6 reduce_sum.19
  (52 shorter events, 13.9 us)
Async XLA Ops:
  0.0 3.9 %slice-start = ((bf16[5,128,1024]{2,1,0:T(8,128)(2,1)}), bf16[1,128,1024]{2,1,0:T(8,128)(2,1)S(1)}, s32[]{:S(2)}) async-start(bf16[5,128,1024]{2,1,0:T(8,128)(2,1)} %param.8), calls=%async_computation.3 | async-start | bytes 524288 | tf_op jit(solution)/shard_map/slice | solution.py:50
  7.1 18.9 %copy-start = (s32[16,128]{1,0:T(8,128)S(1)}, s32[16,128]{1,0:T(8,128)}, u32[]{:S(2)}) copy-start(s32[16,128]{1,0:T(8,128)} %param.12) | copy-start | bytes 24580
  9.0 47.2 %all-to-all-start = ((bf16[2,128,1024]{2,0,1:T(2,128)(2,1)}), bf16[2,128,1024]{2,0,1:T(2,128)(2,1)S(1)}, u32[]{:S(2)}, u32[]{:S(2)}) async-start(bf16[2,128,1024]{2,0,1:T(2,128)(2,1)} %copy.23), calls=%async_computation | async-start | bytes 1048576 | tf_op jit(solution)/shard_map/all_to_all | solution.py:51
  57.2 0.7 copy-start.1
where the time goes:
time: 336 us; the launch traced here: 333 us
  blocking collectives  126 us (38%)
  loops' own time  76.5 us (23%)
  local copies, waits for them, and re-layouts  60.2 us (18%)
  matrix products  22.2 us (7%)
  waiting for transfers between devices  21.9 us (7%)
  starting transfers between devices  17 us (5%)
  other arithmetic  8.99 us (3%)
    all_to_all x1, blocking collectives, summed_on_arrival(): tiles = lax.all_to_all(cut_along(array, dim, count), axis, 0, 0, tiled=True)  102 us
    another operation x1, loops' own time, local(): _, banded = lax.scan(one_band, 0, jnp.arange(band_count, dtype=jnp.int32))  76.5 us
    all_to_all x1, blocking collectives, sum_at_owner(): tiles = lax.all_to_all(cut_along(array, dim, count), axis, 0, 0, tiled=True)  23.6 us
    dot_general x16, matrix products, one_band(): jnp.einsum('kcof,kcft->ot', chosen, windows, preferred_element_type=jnp.f...  22.2 us
    all_to_all x1, waiting for transfers between devices, local(): lax.all_to_all(outgoing, 'cfd', split_axis=1, concat_axis=1, tiled=True)  21.9 us
    another operation x16, local copies, waits for them, and re-layouts, one_band(): jnp.stack([lax.dynamic_slice_in_dim(sources, out_len - delay - shift_step...  17.9 us
    all_to_all x1, starting transfers between devices, local(): lax.all_to_all(outgoing, 'cfd', split_axis=1, concat_axis=1, tiled=True)  17 us
    dynamic_slice x16, local copies, waits for them, and re-layouts, local(): _, banded = lax.scan(one_band, 0, jnp.arange(band_count, dtype=jnp.int32))  9.55 us
  transfers between devices with their start and end apart: 1, of which 1 were waited for; matrix products, arithmetic and copies ran while one was open for 2% of the time, Pallas kernels for 0%

commit v1 on v0

v1 whole, which is shorter than its diff:
```python
import functools

import jax
import jax.numpy as jnp
from jax import lax
from jax.experimental import pallas as pl
from jax.experimental.pallas import tpu as pltpu
from jax.sharding import PartitionSpec as P

MESH = pl.DeviceIdType.MESH
F32 = jnp.float32
BF16 = jnp.bfloat16


def kernel(
    block_map,
    band_observers,
    band_lags,
    surface,
    normals,
    weights_hbm,
    out,
    face_rows,
    staging,
    arrived,
    weights,
    sources,
    product,
    slots,
    rows_tmp,
    inverse_v,
    inverse,
    core_send,
    core_recv,
    send1,
    recv1,
    send2,
    recv2,
    send3,
    recv3,
    weight_sem,
    inverse_sem,
    face_sems,
    core_sems,
    sems1,
    sems2,
    sems3,
):
    cfd = lax.axis_index("cfd")
    ac = lax.axis_index("ac")
    z_lo = cfd // 8
    x = (cfd // 2) % 4
    core = cfd % 2
    y = ac // 2
    z_hi = ac % 2

    def device(z_lo_=z_lo, x_=x, core_=core, y_=y, z_hi_=z_hi):
        return ((z_lo_ * 4 + x_) * 2 + core_, y_ * 2 + z_hi_)

    weight_copy = pltpu.make_async_copy(weights_hbm, weights, weight_sem)
    weight_copy.start()

    barrier = pltpu.get_barrier_semaphore()

    @pl.loop(1, 64)
    def _(offset):
        pl.semaphore_signal(
            barrier, inc=1, device_id=((cfd + offset) % 64, ac), device_id_type=MESH
        )

    for k in range(1, 4):
        pl.semaphore_signal(
            barrier, inc=1, device_id=device(y_=(y + k) % 4), device_id_type=MESH
        )

    for k in range(8):
        pl.semaphore_signal(
            barrier, inc=1, device_id=device(z_lo_=k, z_hi_=1 - z_hi), device_id_type=MESH
        )

    columns = jnp.transpose(
        jnp.concatenate([normals[...].astype(F32), jnp.zeros((5, 128), F32)], axis=0)
    )
    n0, n1, n2 = columns[:, 0:1], columns[:, 1:2], columns[:, 2:3]
    for tile in range(8):
        lanes = pl.ds(tile * 128, 128)
        along = surface[2, :, lanes].astype(F32) * n0
        along = along + surface[3, :, lanes].astype(F32) * n1
        along = along + surface[4, :, lanes].astype(F32) * n2
        face_rows[0, pl.ds(tile, 128, stride=8), :] = surface[1, :, lanes].astype(F32) * along
        face_rows[1, pl.ds(tile, 128, stride=8), :] = surface[0, :, lanes].astype(F32)

    @pl.loop(0, 64, unroll=4)
    def _(d):
        first = block_map[0, 0, d] * 16
        staging[d, pl.ds(0, 16), :] = face_rows[0, pl.ds(first, 16), :].astype(BF16)
        staging[d, pl.ds(16, 16), :] = face_rows[1, pl.ds(first, 16), :].astype(BF16)

    pl.semaphore_wait(barrier, 74)

    def send_block(dest_z, dest_x, dest_core):
        dest = (dest_z * 4 + dest_x) * 2 + dest_core
        pltpu.make_async_remote_copy(
            src_ref=staging.at[dest],
            dst_ref=arrived.at[cfd],
            send_sem=face_sems.at[0],
            recv_sem=face_sems.at[1],
            device_id=(dest, ac),
            device_id_type=MESH,
        ).start()

    @pl.loop(0, 7)
    def _(step):
        dz = 7 - step
        for sign in (1, -1):
            dest_z = z_lo + sign * dz

            @pl.when((dest_z >= 0) & (dest_z < 8))
            def _():
                for k in range(8):
                    send_block(dest_z, (x + k // 2) % 4, (core + k) % 2)

    for k in range(1, 8):
        send_block(z_lo, (x + k // 2) % 4, (core + k) % 2)
    arrived[cfd] = staging[cfd]

    observer = lax.broadcasted_iota(jnp.int32, (16, 128), 0) * 128 + lax.broadcasted_iota(
        jnp.int32, (16, 128), 1
    )

    def find(band, found):
        for m in range(128):
            found = jnp.where(observer == band_observers[band, m], band * 128 + m, found)
        return found

    inverse_v[...] = lax.fori_loop(0, 16, find, jnp.zeros((16, 128), jnp.int32))
    inverse_copy = pltpu.make_async_copy(inverse_v, inverse, inverse_sem)
    inverse_copy.start()
    product[8] = jnp.zeros((2048, 128), F32)
    weight_copy.wait()
    inverse_copy.wait()

    pltpu.make_async_copy(
        arrived.at[pl.ds(0, 63)], staging.at[pl.ds(0, 63)], face_sems.at[1]
    ).wait()

    for series in range(2):
        for part in range(8):
            tile = arrived[pl.ds(part * 8, 8), pl.ds(series * 16, 16), :].astype(F32)
            face_rows[series, pl.ds(part * 128, 128), :] = tile.reshape(128, 128)
    lane = lax.broadcasted_iota(jnp.int32, (128, 128), 1)
    for series in range(2):
        rolled = None
        step_rolled = None
        for tile in range(8):
            lanes = pl.ds(tile * 128, 128)
            now = face_rows[series, pl.ds(tile, 128, stride=8), :]
            turned = pltpu.roll(now, 1, 1)
            before = jnp.where(lane == 0, now if tile == 0 else rolled, turned)
            rolled = turned
            step = (now - before).astype(BF16).astype(F32)
            step_turned = pltpu.roll(step, 1, 1)
            step_before = jnp.where(
                lane == 0, jnp.zeros_like(step) if tile == 0 else step_rolled, step_turned
            )
            step_rolled = step_turned
            sources[pl.ds(series * 128, 128), lanes] = step.astype(BF16)
            sources[pl.ds((3 + series) * 128, 128), lanes] = step_before.astype(BF16)
            if series == 1:
                sources[pl.ds(2 * 128, 128), lanes] = now.astype(BF16)
                sources[pl.ds(5 * 128, 128), lanes] = before.astype(BF16)

    @pl.loop(0, 4)
    def _(n):
        lanes = pl.ds(pl.multiple_of(n * 256, 256), 256)
        for m in range(2):
            rows = pl.ds(m * 1024, 1024)
            left = jnp.concatenate([weights[kc, rows, :] for kc in range(6)], axis=1)
            both = jnp.dot(left, sources[:, lanes], preferred_element_type=F32)
            product[2 * n, rows, :] = both[:, 0:128]
            product[2 * n + 1, rows, :] = both[:, 128:256]

    @pl.loop(0, 16)
    def _(band):
        start = 512 - band_lags[band]
        tile = lax.div(start, 128)
        within = lax.rem(start, 128)
        turn = lax.rem(128 - within, 128)
        rows = pl.ds(pl.multiple_of(band * 128, 128), 128)
        turned = []
        for j in range(5):
            turned.append(pltpu.roll(product[tile + j, rows, :], turn, 1))
            if j > 0:
                slots[pl.ds(band * 512 + j - 1, 128, stride=4), :] = jnp.where(
                    lane < 128 - within, turned[j - 1], turned[j]
                )

    def gather(block_z, block_x, block_core, buffer):
        first = (block_z * 4 + block_x) * 2 + block_core
        for r in range(32):
            slot = inverse[first // 4, (first % 4) * 32 + r]
            rows_tmp[buffer, pl.ds(r * 4, 4), :] = slots[pl.ds(slot * 4, 4), :]
        return [rows_tmp[buffer, pl.ds(j, 32, stride=4), :] for j in range(4)]

    other = 1 - core

    def core_copy(half, index):
        return pltpu.make_async_remote_copy(
            src_ref=core_send.at[half, index],
            dst_ref=core_recv.at[half, index],
            send_sem=core_sems.at[0, half, index],
            recv_sem=core_sems.at[1, half, index],
            device_id=device(core_=other),
            device_id_type=MESH,
        )

    @pl.loop(0, 16)
    def _(step):
        cells = gather(4 + step % 4, step // 4, other, step % 2)
        for j in range(4):
            core_send[1, j, step // 4, step % 4] = cells[j].astype(BF16)

    for k in range(4):
        core_copy(1, (y + 1 + k) % 4).start()
    for k in range(4):
        xk = (x + 1 + k) % 4

        @pl.loop(0, 4)
        def _(step):
            cells = gather(step, xk, other, step % 2)
            for j in range(4):
                core_send[0, xk, j, step] = cells[j].astype(BF16)

        core_copy(0, xk).start()

    def copy1(half, k):
        mine = y if half else x
        target = (mine + k) % 4
        return pltpu.make_async_remote_copy(
            src_ref=send1.at[half, target],
            dst_ref=recv1.at[half, mine],
            send_sem=sems1.at[0, half, k],
            recv_sem=sems1.at[1, half, k],
            device_id=device(y_=target) if half else device(x_=target),
            device_id_type=MESH,
        )

    for k in range(4):
        core_copy(1, (y + 1 + k) % 4).wait_recv()

    @pl.loop(0, 16)
    def _(step):
        cells = gather(4 + step % 4, step // 4, core, step % 2)
        for j in range(4):
            total = cells[j] + core_recv[1, j, step // 4, step % 4].astype(F32)
            send1[1, j, step // 4, step % 4] = total.astype(BF16)

    for k in (2, 1, 3):
        copy1(1, k).start()
    for k in (2, 1, 3, 0):
        xk = (x + k) % 4
        core_copy(0, xk).wait_recv()

        @pl.loop(0, 4)
        def _(step):
            cells = gather(step, xk, core, step % 2)
            for j in range(4):
                total = cells[j] + core_recv[0, xk, j, step].astype(F32)
                send1[0, xk, j, step] = total.astype(BF16)

        if k:
            copy1(0, k).start()

    def received1(half, k):
        mine = y if half else x
        source = (mine + 4 - k) % 4
        return pltpu.make_async_remote_copy(
            src_ref=send1.at[half, source],
            dst_ref=recv1.at[half, source],
            send_sem=sems1.at[0, half, k],
            recv_sem=sems1.at[1, half, k],
            device_id=device(y_=source) if half else device(x_=source),
            device_id_type=MESH,
        )

    def copy2(half, k):
        mine = x if half else y
        target = (mine + k) % 4
        return pltpu.make_async_remote_copy(
            src_ref=send2.at[half, target],
            dst_ref=recv2.at[half, mine],
            send_sem=sems2.at[0, half, k],
            recv_sem=sems2.at[1, half, k],
            device_id=device(x_=target) if half else device(y_=target),
            device_id_type=MESH,
        )

    def received2(half, k):
        mine = x if half else y
        source = (mine + 4 - k) % 4
        return pltpu.make_async_remote_copy(
            src_ref=send2.at[half, source],
            dst_ref=recv2.at[half, source],
            send_sem=sems2.at[0, half, k],
            recv_sem=sems2.at[1, half, k],
            device_id=device(x_=source) if half else device(y_=source),
            device_id_type=MESH,
        )

    for half in (1, 0):
        mine = y if half else x
        other_axis = x if half else y
        for k in (1, 3, 2):
            received1(half, k).wait_recv()
        for k in (2, 1, 3, 0):
            index = (other_axis + k) % 4
            for cell in range(4):
                total = send1[half, mine, index, cell].astype(F32)
                for s in range(1, 4):
                    total = total + recv1[half, (mine + s) % 4, index, cell].astype(F32)
                send2[half, index, cell] = total.astype(BF16)
            if k:
                copy2(half, k).start()

    z = z_hi * 8 + z_lo
    lane16 = lax.broadcasted_iota(jnp.int32, (16, 128), 1)
    for half in (1, 0):
        mine = x if half else y
        for k in (1, 3, 2):
            received2(half, k).wait_recv()
        for cell in range(4):
            total = send2[half, mine, cell].astype(F32)
            for s in range(1, 4):
                total = total + recv2[half, (mine + s) % 4, cell].astype(F32)
            top, bottom = total[0:16], total[16:32]
            send3[half * 4 + cell] = jnp.where(
                lane16 < 64, top, pltpu.roll(bottom, 64, 1)
            ).astype(BF16)
            send3[8 + half * 4 + cell] = jnp.where(
                lane16 < 64, pltpu.roll(top, 64, 1), bottom
            ).astype(BF16)

    def copy3(k):
        target = (z + k) % 16
        return pltpu.make_async_remote_copy(
            src_ref=send3.at[target],
            dst_ref=recv3.at[z],
            send_sem=sems3.at[0, k],
            recv_sem=sems3.at[1, k],
            device_id=device(z_lo_=target % 8, z_hi_=target // 8),
            device_id_type=MESH,
        )

    def received3(k):
        source = (z + 16 - k) % 16
        return pltpu.make_async_remote_copy(
            src_ref=send3.at[source],
            dst_ref=recv3.at[source],
            send_sem=sems3.at[0, k],
            recv_sem=sems3.at[1, k],
            device_id=device(z_lo_=source % 8, z_hi_=source // 8),
            device_id_type=MESH,
        )

    for k in (8, 7, 9, 6, 10, 5, 11, 4, 12, 3, 13, 2, 14, 1, 15):
        copy3(k).start()
    total = send3[z].astype(F32)
    for k in (1, 15, 2, 14, 3, 13, 4, 12, 5, 11, 6, 10, 7, 9, 8):
        received3(k).wait_recv()
        total = total + recv3[(z + 16 - k) % 16].astype(F32)
    out[pl.ds(0, 16), :] = total[:, 0:64]
    out[pl.ds(16, 16), :] = total[:, 64:128]

    pltpu.make_async_copy(
        staging.at[pl.ds(0, 63)], arrived.at[pl.ds(0, 63)], face_sems.at[0]
    ).wait()
    for half in range(2):
        for k in range(4):
            core_copy(half, k).wait_send()
        for k in range(1, 4):
            copy1(half, k).wait_send()
            copy2(half, k).wait_send()
    for k in range(1, 16):
        copy3(k).wait_send()


def local(surface_raw, area_normals, kernel_weights, block_map, band_observers, band_lags):
    smem = pl.BlockSpec(memory_space=pltpu.SMEM)
    vmem = pl.BlockSpec(memory_space=pltpu.VMEM)
    weights = kernel_weights.reshape(6, 2048, 128)
    dma = pltpu.SemaphoreType.DMA
    return pl.pallas_call(
        kernel,
        out_shape=jax.ShapeDtypeStruct((32, 64), F32),
        in_specs=[smem, smem, smem, vmem, vmem, pl.BlockSpec(memory_space=pl.ANY)],
        out_specs=vmem,
        scratch_shapes=[
            pltpu.VMEM((2, 1024, 128), F32),
            pltpu.VMEM((64, 32, 128), BF16),
            pltpu.VMEM((64, 32, 128), BF16),
            pltpu.VMEM((6, 2048, 128), BF16),
            pltpu.VMEM((768, 1024), BF16),
            pltpu.VMEM((9, 2048, 128), F32),
            pltpu.VMEM((8192, 128), F32),
            pltpu.VMEM((2, 128, 128), F32),
            pltpu.VMEM((16, 128), jnp.int32),
            pltpu.SMEM((16, 128), jnp.int32),
            pltpu.VMEM((2, 4, 4, 4, 32, 128), BF16),
            pltpu.VMEM((2, 4, 4, 4, 32, 128), BF16),
            pltpu.VMEM((2, 4, 4, 4, 32, 128), BF16),
            pltpu.VMEM((2, 4, 4, 4, 32, 128), BF16),
            pltpu.VMEM((2, 4, 4, 32, 128), BF16),
            pltpu.VMEM((2, 4, 4, 32, 128), BF16),
            pltpu.VMEM((16, 16, 128), BF16),
            pltpu.VMEM((16, 16, 128), BF16),
            dma,
            dma,
            dma((2,)),
            dma((2, 2, 4)),
            dma((2, 2, 4)),
            dma((2, 2, 4)),
            dma((2, 16)),
        ],
        compiler_params=pltpu.CompilerParams(collective_id=0, has_side_effects=True),
    )(block_map, band_observers, band_lags, surface_raw, area_normals, weights)


def solution(mesh):
    placed = (
        P(None, ("cfd", "ac"), None),
        P(None, ("cfd", "ac")),
        P(None, None, None, ("cfd", "ac")),
        P("ac", "cfd", None),
        P(),
        P(),
    )
    return jax.shard_map(
        local, mesh=mesh, in_specs=placed, out_specs=P("cfd", "ac"), check_vma=False
    )
```

time: 336 us -> 78.1 us (0.23)
  blocking collectives: 126 us -> 0 us
  Pallas kernels: 0 us -> 76.5 us
  loops' own time: 76.5 us -> 0 us
  local copies, waits for them, and re-layouts: 60.2 us -> 1.32 us
  matrix products: 22.2 us -> 0 us
  waiting for transfers between devices: 21.9 us -> 0 us
  starting transfers between devices: 17 us -> 0 us
  other arithmetic: 8.99 us -> 0 us
    all_to_all x2 -> x0, blocking collectives: 126 us -> none  [the longest x1 102 us: summed_on_arrival(): tiles = lax.all_to_all(cut_along(array, dim, count), axis, 0, 0, tiled=True)]
    another operation x1 -> x0, loops' own time: 76.5 us -> none  [local(): _, banded = lax.scan(one_band, 0, jnp.arange(band_count, dtype=jnp.int32))]
    pallas_call x0 -> x1, Pallas kernels: none -> 76.5 us  [local(): pl.pallas_call(kernel, out_shape=jax.ShapeDtypeStruct((32, 64), F32), in_...]
    dot_general x16 -> x0, matrix products: 22.2 us -> none  [one_band(): jnp.einsum('kcof,kcft->ot', chosen, windows, preferred_element_type=jnp.f...]
    all_to_all x1 -> x0, waiting for transfers between devices: 21.9 us -> none  [local(): lax.all_to_all(outgoing, 'cfd', split_axis=1, concat_axis=1, tiled=True)]
    dynamic_slice x32 -> x0, local copies, waits for them, and re-layouts: 18.8 us -> none  [the longest x16 9.55 us: local(): _, banded = lax.scan(one_band, 0, jnp.arange(band_count, dtype=jnp.int32))]
    another operation x19 -> x0, local copies, waits for them, and re-layouts: 18.7 us -> none  [the longest x16 17.9 us: one_band(): jnp.stack([lax.dynamic_slice_in_dim(sources, out_len - delay - shift_step...]
    all_to_all x1 -> x0, starting transfers between devices: 17 us -> none  [local(): lax.all_to_all(outgoing, 'cfd', split_axis=1, concat_axis=1, tiled=True)]
  transfers between devices with their start and end apart: 1 -> 0, of which waited for: 1 -> 0; matrix products, arithmetic and copies ran while one was open for 2% -> 0% of each run, Pallas kernels for 0% -> 0%
where the time goes in v1:
time: 78.1 us; the launch traced here: 77.8 us
  Pallas kernels  76.5 us (98%)
  local copies, waits for them, and re-layouts  1.32 us (2%)
    pallas_call x1, Pallas kernels, local(): pl.pallas_call(kernel, out_shape=jax.ShapeDtypeStruct((32, 64), F32), in_...  76.5 us

profile of v1, /device:TPU:1, one launch (start us, length us, event | category | flops | bytes accessed | tf_op | source)
XLA Modules:
  0.0 77.8 jit_solution(8037349701323121109)
XLA Ops:
  0.0 76.5 %shard_map.64 = f32[32,64]{1,0:T(8,128)} custom-call(s32[1,1,64]{2,1,0:T(1,128)} %block_map.1, s32[16,128]{1,0:T(8,128)} %band_observers.1, s32[16]{0:T(128)} %band_lags.1, bf16[5,128,1024]{2,1,0:T(8,128)(2,1)} %surface.1, bf16[3,128]{1,0:T(4,128)(2,1)} %normals.1, bf16[6,2048,128]{2,1,0:T(8,128)(2,1)} %bitcast.1), custom_call_target="tpu_custom_call" | custom-call | tf_op jit(solution)/shard_map/pallas_call | solution.py:392
  76.5 1.3 %copy.8 = f32[32,64]{1,0:T(8,128)} copy(f32[32,64]{1,0:T(8,128)} %shard_map.64) | data formatting | bytes 16384

commit v2 on v0

v2 whole, which is shorter than its diff:
```python
import functools

import jax
import jax.numpy as jnp
from jax import lax
from jax.experimental import pallas as pl
from jax.experimental.pallas import tpu as pltpu
from jax.sharding import PartitionSpec as P

MESH = pl.DeviceIdType.MESH
F32 = jnp.float32
BF16 = jnp.bfloat16

PITCH = 9


def kernel(
    block_map,
    band_observers,
    band_lags,
    surface,
    normals,
    weights_hbm,
    out,
    face_rows,
    staging,
    arrived,
    weights,
    pressure_sources,
    thickness_sources,
    product,
    slots,
    rows_tmp,
    table_v,
    table,
    core_send,
    core_recv,
    send1,
    recv1,
    send2,
    recv2,
    send3,
    recv3,
    weight_sem,
    table_sem,
    face_sems,
    core_sems,
    sems1,
    sems2,
    sems3,
):
    cfd = lax.axis_index("cfd")
    ac = lax.axis_index("ac")
    z_lo = cfd // 8
    x = (cfd // 2) % 4
    core = cfd % 2
    y = ac // 2
    z_hi = ac % 2
    z = z_hi * 8 + z_lo

    def device(z_lo_=z_lo, x_=x, core_=core, y_=y, z_hi_=z_hi):
        return ((z_lo_ * 4 + x_) * 2 + core_, y_ * 2 + z_hi_)

    weight_copy = pltpu.make_async_copy(weights_hbm, weights, weight_sem)
    weight_copy.start()

    barrier = pltpu.get_barrier_semaphore()

    @pl.loop(1, 64)
    def _(offset):
        pl.semaphore_signal(
            barrier, inc=1, device_id=((cfd + offset) % 64, ac), device_id_type=MESH
        )

    for k in range(1, 4):
        pl.semaphore_signal(
            barrier, inc=1, device_id=device(y_=(y + k) % 4), device_id_type=MESH
        )

    for k in range(8):
        pl.semaphore_signal(
            barrier, inc=1, device_id=device(z_lo_=k, z_hi_=1 - z_hi), device_id_type=MESH
        )

    columns = jnp.transpose(
        jnp.concatenate([normals[...].astype(F32), jnp.zeros((5, 128), F32)], axis=0)
    )
    n0, n1, n2 = columns[:, 0:1], columns[:, 1:2], columns[:, 2:3]
    for tile in range(8):
        lanes = pl.ds(tile * 128, 128)
        along = surface[2, :, lanes].astype(F32) * n0
        along = along + surface[3, :, lanes].astype(F32) * n1
        along = along + surface[4, :, lanes].astype(F32) * n2
        face_rows[1, pl.ds(tile, 128, stride=8), :] = surface[1, :, lanes].astype(F32) * along
        face_rows[0, pl.ds(tile, 128, stride=8), :] = surface[0, :, lanes].astype(F32)

    @pl.loop(0, 64, unroll=4)
    def _(d):
        first = block_map[0, 0, d] * 16
        for series in range(2):
            staging[series, d] = face_rows[series, pl.ds(first, 16), :].astype(BF16)

    pl.semaphore_wait(barrier, 74)

    def send_block(series, dest_z, k):
        dest = (dest_z * 4 + (x + k // 2) % 4) * 2 + (core + k) % 2
        pltpu.make_async_remote_copy(
            src_ref=staging.at[series, dest],
            dst_ref=arrived.at[series, cfd],
            send_sem=face_sems.at[0, series],
            recv_sem=face_sems.at[1, series],
            device_id=(dest, ac),
            device_id_type=MESH,
        ).start()

    for series in range(2):

        @pl.loop(0, 7)
        def _(step):
            dz = 7 - step
            for sign in (1, -1):
                dest_z = z_lo + sign * dz

                @pl.when((dest_z >= 0) & (dest_z < 8))
                def _():
                    for k in range(8):
                        send_block(series, dest_z, k)

        for k in range(1, 8):
            send_block(series, z_lo, k)
        arrived[series, cfd] = staging[series, cfd]

    observer = lax.broadcasted_iota(jnp.int32, (64, 128), 0) * 32 + (
        lax.broadcasted_iota(jnp.int32, (64, 128), 1) % 32
    )

    def find(band, found):
        start = 511 - band_lags[band]
        row = band * (128 * PITCH) + lax.div(start, 128)
        code = row * 128 + 127 - lax.rem(start, 128)
        for m in range(128):
            found = jnp.where(
                observer == band_observers[band, m], code + m * PITCH * 128, found
            )
        return found

    table_v[...] = lax.fori_loop(0, 16, find, jnp.zeros((64, 128), jnp.int32))
    table_copy = pltpu.make_async_copy(table_v, table, table_sem)
    table_copy.start()
    weight_copy.wait()
    table_copy.wait()

    def faces_arrived(series):
        pltpu.make_async_copy(
            arrived.at[series, pl.ds(0, 63)],
            staging.at[series, pl.ds(0, 63)],
            face_sems.at[1, series],
        ).wait()
        for part in range(8):
            tile = arrived[series, pl.ds(part * 8, 8)].astype(F32)
            face_rows[series, pl.ds(part * 128, 128), :] = tile.reshape(128, 128)

    lane = lax.broadcasted_iota(jnp.int32, (128, 128), 1)

    def differences(series):
        rolled = None
        step_rolled = None
        for tile in range(8):
            now = face_rows[series, pl.ds(tile, 128, stride=8), :]
            turned = pltpu.roll(now, 1, 1)
            before = jnp.where(lane == 0, now if tile == 0 else rolled, turned)
            rolled = turned
            step = (now - before).astype(BF16).astype(F32)
            step_turned = pltpu.roll(step, 1, 1)
            step_before = jnp.where(
                lane == 0, jnp.zeros_like(step) if tile == 0 else step_rolled, step_turned
            )
            step_rolled = step_turned
            yield (
                pl.ds(tile * 128, 128),
                [value.astype(BF16) for value in (now, before, step, step_before)],
            )

    faces_arrived(0)
    for lanes, (now, before, step, step_before) in differences(0):
        for row, value in enumerate((step, now, step_before, before)):
            pressure_sources[pl.ds(row * 128, 128), lanes] = value

    @pl.loop(0, 4)
    def _(n):
        lanes = pl.ds(pl.multiple_of(n * 256, 256), 256)
        for m in range(2):
            rows = pl.ds(m * 1024, 1024)
            left = jnp.concatenate([weights[kc, rows, :] for kc in (1, 2, 4, 5)], axis=1)
            both = jnp.dot(left, pressure_sources[:, lanes], preferred_element_type=F32)
            product[2 * n, rows, :] = both[:, 0:128]
            product[2 * n + 1, rows, :] = both[:, 128:256]

    faces_arrived(1)
    for lanes, (now, before, step, step_before) in differences(1):
        thickness_sources[pl.ds(0, 128), lanes] = step
        thickness_sources[pl.ds(128, 128), lanes] = step_before

    @pl.loop(0, 4)
    def _(n):
        lanes = pl.ds(pl.multiple_of(n * 256, 256), 256)
        for m in range(2):
            rows = pl.ds(m * 1024, 1024)
            left = jnp.concatenate([weights[kc, rows, :] for kc in (0, 3)], axis=1)
            both = jnp.dot(left, thickness_sources[:, lanes], preferred_element_type=F32)
            for side in range(2):
                slots[pl.ds(m * 1024 * PITCH + 2 * n + side, 1024, stride=PITCH), :] = (
                    product[2 * n + side, rows, :] + both[:, side * 128 : side * 128 + 128]
                )

    lane4 = lax.broadcasted_iota(jnp.int32, (4, 128), 1)
    lane16 = lax.broadcasted_iota(jnp.int32, (16, 128), 1)

    def gather(half, block_x, block_core):
        for n in range(4):
            first = (((z + 5 + 2 * n + half) % 8) * 4 + block_x) * 2 + block_core
            for r in range(32):
                code = table[first, r]
                row = lax.shift_right_logical(code, 7)
                turn = code & 127
                rows_tmp[n, pl.ds(r * 4, 4), :] = jnp.where(
                    lane4 < turn,
                    pltpu.roll(slots[pl.ds(row, 4), :], turn, 1),
                    pltpu.roll(slots[pl.ds(row + 1, 4), :], turn, 1),
                )
        for n in range(4):
            chunk = ((z + 5 + 2 * n + half) % 16) // 8
            for j in range(4):
                top = rows_tmp[n, pl.ds(j, 16, stride=4), :]
                bottom = rows_tmp[n, pl.ds(64 + j, 16, stride=4), :]
                yield (
                    (chunk, j, n),
                    jnp.where(lane16 < 64, top, pltpu.roll(bottom, 64, 1)),
                )
                yield (
                    (1 - chunk, j, n),
                    jnp.where(lane16 < 64, pltpu.roll(top, 64, 1), bottom),
                )

    other = 1 - core

    def core_copy(half, chunk):
        return pltpu.make_async_remote_copy(
            src_ref=core_send.at[half, chunk],
            dst_ref=core_recv.at[half, chunk],
            send_sem=core_sems.at[0, half, chunk],
            recv_sem=core_sems.at[1, half, chunk],
            device_id=device(core_=other),
            device_id_type=MESH,
        )

    def spot(half, chunk, xk, j, n):
        return (half, chunk, j, xk, n) if half else (half, chunk, xk, j, n)

    for half in (1, 0):

        @pl.loop(0, 4)
        def _(xk):
            for (chunk, j, n), tile in gather(half, xk, other):
                core_send[spot(half, chunk, xk, j, n)] = tile.astype(BF16)

        for chunk in range(2):
            core_copy(half, chunk).start()

    def copies(stage, half, chunk, k, arriving):
        along_y = half == (stage == 1)
        mine = y if along_y else x
        peer = (mine + (4 - k if arriving else k)) % 4
        source, landing, sems = (send1, recv1, sems1) if stage == 1 else (send2, recv2, sems2)
        return pltpu.make_async_remote_copy(
            src_ref=source.at[half, chunk, peer],
            dst_ref=landing.at[half, chunk, peer if arriving else mine],
            send_sem=sems.at[0, half, chunk, k],
            recv_sem=sems.at[1, half, chunk, k],
            device_id=device(y_=peer) if along_y else device(x_=peer),
            device_id_type=MESH,
        )

    for half in (1, 0):
        for chunk in range(2):
            core_copy(half, chunk).wait_recv()

        @pl.loop(0, 4)
        def _(xk):
            for (chunk, j, n), tile in gather(half, xk, core):
                at = spot(half, chunk, xk, j, n)
                send1[at] = (tile + core_recv[at].astype(F32)).astype(BF16)

        for chunk in range(2):
            for k in (2, 1, 3):
                copies(1, half, chunk, k, False).start()

    def second(half, chunk):
        mine, across = (y, x) if half else (x, y)
        for k in (1, 3, 2):
            copies(1, half, chunk, k, True).wait_recv()
        for k in (2, 1, 3, 0):
            index = (across + k) % 4
            for n in range(4):
                total = send1[half, chunk, mine, index, n].astype(F32)
                for s in range(1, 4):
                    total = total + recv1[half, chunk, (mine + s) % 4, index, n].astype(F32)
                send2[half, chunk, index, n] = total.astype(BF16)
            if k:
                copies(2, half, chunk, k, False).start()

    def copy3(i, arriving):
        dz = (5 + i) % 16
        peer = (z + (16 - dz if arriving else dz)) % 16
        return pltpu.make_async_remote_copy(
            src_ref=send3.at[i],
            dst_ref=recv3.at[i],
            send_sem=sems3.at[0, i],
            recv_sem=sems3.at[1, i],
            device_id=device(z_lo_=peer % 8, z_hi_=peer // 8),
            device_id_type=MESH,
        )

    def third(half, chunk):
        mine = x if half else y
        for k in (1, 3, 2):
            copies(2, half, chunk, k, True).wait_recv()
        for n in ((2, 1, 3, 0), (1, 2, 0, 3))[half]:
            total = send2[half, chunk, mine, n].astype(F32)
            for s in range(1, 4):
                total = total + recv2[half, chunk, (mine + s) % 4, n].astype(F32)
            i = chunk * 8 + 2 * n + half
            send3[i] = total.astype(BF16)
            if i != 11:
                copy3(i, False).start()

    for chunk in range(2):
        for half in (1, 0):
            second(half, chunk)
        for half in (1, 0):
            third(half, chunk)

    total = send3[11].astype(F32)
    for i in (10, 12, 9, 13, 8, 14, 15, 7, 0, 6, 1, 5, 2, 4, 3):
        copy3(i, True).wait_recv()
        total = total + recv3[i].astype(F32)
    out[pl.ds(0, 16), :] = total[:, 0:64]
    out[pl.ds(16, 16), :] = total[:, 64:128]

    for series in range(2):
        pltpu.make_async_copy(
            staging.at[series, pl.ds(0, 63)],
            arrived.at[series, pl.ds(0, 63)],
            face_sems.at[0, series],
        ).wait()
    for half in range(2):
        for chunk in range(2):
            core_copy(half, chunk).wait_send()
            for k in range(1, 4):
                copies(1, half, chunk, k, False).wait_send()
                copies(2, half, chunk, k, False).wait_send()
    for i in range(16):
        if i != 11:
            copy3(i, False).wait_send()


def local(surface_raw, area_normals, kernel_weights, block_map, band_observers, band_lags):
    smem = pl.BlockSpec(memory_space=pltpu.SMEM)
    vmem = pl.BlockSpec(memory_space=pltpu.VMEM)
    weights = kernel_weights.reshape(6, 2048, 128)
    dma = pltpu.SemaphoreType.DMA
    return pl.pallas_call(
        kernel,
        out_shape=jax.ShapeDtypeStruct((32, 64), F32),
        in_specs=[smem, smem, smem, vmem, vmem, pl.BlockSpec(memory_space=pl.ANY)],
        out_specs=vmem,
        scratch_shapes=[
            pltpu.VMEM((2, 1024, 128), F32),
            pltpu.VMEM((2, 64, 16, 128), BF16),
            pltpu.VMEM((2, 64, 16, 128), BF16),
            pltpu.VMEM((6, 2048, 128), BF16),
            pltpu.VMEM((512, 1024), BF16),
            pltpu.VMEM((256, 1024), BF16),
            pltpu.VMEM((8, 2048, 128), F32),
            pltpu.VMEM((2048 * PITCH, 128), F32),
            pltpu.VMEM((4, 128, 128), F32),
            pltpu.VMEM((64, 128), jnp.int32),
            pltpu.SMEM((64, 128), jnp.int32),
            pltpu.VMEM((2, 2, 4, 4, 4, 16, 128), BF16),
            pltpu.VMEM((2, 2, 4, 4, 4, 16, 128), BF16),
            pltpu.VMEM((2, 2, 4, 4, 4, 16, 128), BF16),
            pltpu.VMEM((2, 2, 4, 4, 4, 16, 128), BF16),
            pltpu.VMEM((2, 2, 4, 4, 16, 128), BF16),
            pltpu.VMEM((2, 2, 4, 4, 16, 128), BF16),
            pltpu.VMEM((16, 16, 128), BF16),
            pltpu.VMEM((16, 16, 128), BF16),
            dma,
            dma,
            dma((2, 2)),
            dma((2, 2, 2)),
            dma((2, 2, 2, 4)),
            dma((2, 2, 2, 4)),
            dma((2, 16)),
        ],
        compiler_params=pltpu.CompilerParams(collective_id=0, has_side_effects=True),
    )(block_map, band_observers, band_lags, surface_raw, area_normals, weights)


def solution(mesh):
    placed = (
        P(None, ("cfd", "ac"), None),
        P(None, ("cfd", "ac")),
        P(None, None, None, ("cfd", "ac")),
        P("ac", "cfd", None),
        P(),
        P(),
    )
    return jax.shard_map(
        local, mesh=mesh, in_specs=placed, out_specs=P("cfd", "ac"), check_vma=False
    )
```

time: 336 us -> 74.8 us (0.22)
  the two profiles are of different devices: /device:TPU:1 before, /device:TPU:32 now
where the time goes in v2:
time: 74.8 us; the launch traced here: 74.5 us
  Pallas kernels  73.2 us (98%)
  local copies, waits for them, and re-layouts  1.32 us (2%)
    pallas_call x1, Pallas kernels, local(): pl.pallas_call(kernel, out_shape=jax.ShapeDtypeStruct((32, 64), F32), in_...  73.2 us

profile of v2, /device:TPU:32, one launch (start us, length us, event | category | flops | bytes accessed | tf_op | source)
XLA Modules:
  0.0 74.5 jit_solution(13090929007003676657)
XLA Ops:
  0.0 73.2 %shard_map.64 = f32[32,64]{1,0:T(8,128)} custom-call(s32[1,1,64]{2,1,0:T(1,128)} %block_map.1, s32[16,128]{1,0:T(8,128)} %band_observers.1, s32[16]{0:T(128)} %band_lags.1, bf16[5,128,1024]{2,1,0:T(8,128)(2,1)} %surface.1, bf16[3,128]{1,0:T(4,128)(2,1)} %normals.1, bf16[6,2048,128]{2,1,0:T(8,128)(2,1)} %bitcast.1), custom_call_target="tpu_custom_call" | custom-call | tf_op jit(solution)/shard_map/pallas_call | solution.py:372
  73.2 1.3 %copy.8 = f32[32,64]{1,0:T(8,128)} copy(f32[32,64]{1,0:T(8,128)} %shard_map.64) | data formatting | bytes 16384

commit v3 on v2

--- a/solution.py
+++ b/solution.py
@@ -15,13 +15,18 @@
 
 
 def kernel(
+    block_map_hbm,
+    band_observers_hbm,
+    band_lags_hbm,
+    surface_hbm,
+    normals_hbm,
+    weights_hbm,
+    out,
     block_map,
     band_observers,
     band_lags,
     surface,
     normals,
-    weights_hbm,
-    out,
     face_rows,
     staging,
     arrived,
@@ -41,7 +46,8 @@
     recv2,
     send3,
     recv3,
-    weight_sem,
+    round_sem,
+    input_sems,
     table_sem,
     face_sems,
     core_sems,
@@ -61,26 +67,42 @@
     def device(z_lo_=z_lo, x_=x, core_=core, y_=y, z_hi_=z_hi):
         return ((z_lo_ * 4 + x_) * 2 + core_, y_ * 2 + z_hi_)
 
-    weight_copy = pltpu.make_async_copy(weights_hbm, weights, weight_sem)
-    weight_copy.start()
-
     barrier = pltpu.get_barrier_semaphore()
 
-    @pl.loop(1, 64)
-    def _(offset):
-        pl.semaphore_signal(
-            barrier, inc=1, device_id=((cfd + offset) % 64, ac), device_id_type=MESH
-        )
-
+    for dz in (4, -4, 3, -3, 2, -2, 1, -1, 0):
+        there = (z + 16 + dz) % 16
+        for k in range(8):
+            if dz or k:
+                pl.semaphore_signal(
+                    barrier,
+                    inc=1,
+                    device_id=device(
+                        there % 8, (x + k // 2) % 4, (core + k) % 2, y, there // 8
+                    ),
+                    device_id_type=MESH,
+                )
     for k in range(1, 4):
         pl.semaphore_signal(
             barrier, inc=1, device_id=device(y_=(y + k) % 4), device_id_type=MESH
         )
 
-    for k in range(8):
-        pl.semaphore_signal(
-            barrier, inc=1, device_id=device(z_lo_=k, z_hi_=1 - z_hi), device_id_type=MESH
-        )
+    inputs = [
+        pltpu.make_async_copy(source, copy, input_sems.at[n])
+        for n, (source, copy) in enumerate(
+            (
+                (surface_hbm, surface),
+                (normals_hbm, normals),
+                (block_map_hbm, block_map),
+                (band_lags_hbm, band_lags),
+                (band_observers_hbm, band_observers),
+                (weights_hbm, weights),
+            )
+        )
+    ]
+    for copy in inputs:
+        copy.start()
+    for copy in inputs[:3]:
+        copy.wait()
 
     columns = jnp.transpose(
         jnp.concatenate([normals[...].astype(F32), jnp.zeros((5, 128), F32)], axis=0)
@@ -101,6 +123,14 @@
             staging[series, d] = face_rows[series, pl.ds(first, 16), :].astype(BF16)
 
     pl.semaphore_wait(barrier, 74)
+    for dz in (4, -4):
+        there = (z + 16 + dz) % 16
+        pl.semaphore_signal(
+            round_sem,
+            inc=1,
+            device_id=device(z_lo_=there % 8, z_hi_=there // 8),
+            device_id_type=MESH,
+        )
 
     def send_block(series, dest_z, k):
         dest = (dest_z * 4 + (x + k // 2) % 4) * 2 + (core + k) % 2
@@ -113,11 +143,10 @@
             device_id_type=MESH,
         ).start()
 
-    for series in range(2):
-
-        @pl.loop(0, 7)
+    def send_far_to_near(series, farthest, nearest):
+        @pl.loop(0, farthest - nearest + 1)
         def _(step):
-            dz = 7 - step
+            dz = farthest - step
             for sign in (1, -1):
                 dest_z = z_lo + sign * dz
 
@@ -126,9 +155,19 @@
                     for k in range(8):
                         send_block(series, dest_z, k)
 
-        for k in range(1, 8):
-            send_block(series, z_lo, k)
+    send_far_to_near(0, 4, 1)
+    pl.semaphore_wait(round_sem, 2)
+    send_far_to_near(0, 7, 5)
+    for k in range(1, 8):
+        send_block(0, z_lo, k)
+    send_far_to_near(1, 7, 1)
+    for k in range(1, 8):
+        send_block(1, z_lo, k)
+    for series in range(2):
         arrived[series, cfd] = staging[series, cfd]
+
+    for copy in inputs[3:]:
+        copy.wait()
 
     observer = lax.broadcasted_iota(jnp.int32, (64, 128), 0) * 32 + (
         lax.broadcasted_iota(jnp.int32, (64, 128), 1) % 32
@@ -147,7 +186,6 @@
     table_v[...] = lax.fori_loop(0, 16, find, jnp.zeros((64, 128), jnp.int32))
     table_copy = pltpu.make_async_copy(table_v, table, table_sem)
     table_copy.start()
-    weight_copy.wait()
     table_copy.wait()
 
     def faces_arrived(series):
@@ -201,7 +239,7 @@
         thickness_sources[pl.ds(0, 128), lanes] = step
         thickness_sources[pl.ds(128, 128), lanes] = step_before
 
-    @pl.loop(0, 4)
+    @pl.loop(0, 4, unroll=4)
     def _(n):
         lanes = pl.ds(pl.multiple_of(n * 256, 256), 256)
         for m in range(2):
@@ -213,34 +251,35 @@
                     product[2 * n + side, rows, :] + both[:, side * 128 : side * 128 + 128]
                 )
 
-    lane4 = lax.broadcasted_iota(jnp.int32, (4, 128), 1)
+    back4 = 127 - lax.broadcasted_iota(jnp.int32, (4, 128), 1)
     lane16 = lax.broadcasted_iota(jnp.int32, (16, 128), 1)
 
     def gather(half, block_x, block_core):
-        for n in range(4):
-            first = (((z + 5 + 2 * n + half) % 8) * 4 + block_x) * 2 + block_core
-            for r in range(32):
-                code = table[first, r]
-                row = lax.shift_right_logical(code, 7)
-                turn = code & 127
-                rows_tmp[n, pl.ds(r * 4, 4), :] = jnp.where(
-                    lane4 < turn,
-                    pltpu.roll(slots[pl.ds(row, 4), :], turn, 1),
-                    pltpu.roll(slots[pl.ds(row + 1, 4), :], turn, 1),
-                )
-        for n in range(4):
-            chunk = ((z + 5 + 2 * n + half) % 16) // 8
-            for j in range(4):
-                top = rows_tmp[n, pl.ds(j, 16, stride=4), :]
-                bottom = rows_tmp[n, pl.ds(64 + j, 16, stride=4), :]
-                yield (
-                    (chunk, j, n),
-                    jnp.where(lane16 < 64, top, pltpu.roll(bottom, 64, 1)),
-                )
-                yield (
-                    (1 - chunk, j, n),
-                    jnp.where(lane16 < 64, pltpu.roll(top, 64, 1), bottom),
-                )
+        for n in range(5):
+            if n < 4:
+                first = (((z + 5 + 2 * n + half) % 8) * 4 + block_x) * 2 + block_core
+                for r in range(32):
+                    code = table[first, r]
+                    row = lax.shift_right_logical(code, 7)
+                    turn = code & 127
+                    picked = jnp.where(
+                        back4 < turn, slots[pl.ds(row, 4), :], slots[pl.ds(row + 1, 4), :]
+                    )
+                    rows_tmp[n, pl.ds(r * 4, 4), :] = pltpu.roll(picked, turn, 1)
+            if n > 0:
+                m = n - 1
+                chunk = ((z + 5 + 2 * m + half) % 16) // 8
+                for j in range(4):
+                    top = rows_tmp[m, pl.ds(j, 16, stride=4), :]
+                    bottom = rows_tmp[m, pl.ds(64 + j, 16, stride=4), :]
+                    yield (
+                        (chunk, j, m),
+                        jnp.where(lane16 < 64, top, pltpu.roll(bottom, 64, 1)),
+                    )
+                    yield (
+                        (1 - chunk, j, m),
+                        jnp.where(lane16 < 64, pltpu.roll(top, 64, 1), bottom),
+                    )
 
     other = 1 - core
 
@@ -259,7 +298,7 @@
 
     for half in (1, 0):
 
-        @pl.loop(0, 4)
+        @pl.loop(0, 4, unroll=2)
         def _(xk):
             for (chunk, j, n), tile in gather(half, xk, other):
                 core_send[spot(half, chunk, xk, j, n)] = tile.astype(BF16)
@@ -285,7 +324,7 @@
         for chunk in range(2):
             core_copy(half, chunk).wait_recv()
 
-        @pl.loop(0, 4)
+        @pl.loop(0, 4, unroll=2)
         def _(xk):
             for (chunk, j, n), tile in gather(half, xk, core):
                 at = spot(half, chunk, xk, j, n)
@@ -365,16 +404,20 @@
 
 
 def local(surface_raw, area_normals, kernel_weights, block_map, band_observers, band_lags):
-    smem = pl.BlockSpec(memory_space=pltpu.SMEM)
-    vmem = pl.BlockSpec(memory_space=pltpu.VMEM)
+    anywhere = pl.BlockSpec(memory_space=pl.ANY)
     weights = kernel_weights.reshape(6, 2048, 128)
     dma = pltpu.SemaphoreType.DMA
     return pl.pallas_call(
         kernel,
         out_shape=jax.ShapeDtypeStruct((32, 64), F32),
-        in_specs=[smem, smem, smem, vmem, vmem, pl.BlockSpec(memory_space=pl.ANY)],
-        out_specs=vmem,
+        in_specs=[anywhere] * 6,
+        out_specs=pl.BlockSpec(memory_space=pltpu.VMEM),
         scratch_shapes=[
+            pltpu.SMEM((1, 1, 64), jnp.int32),
+            pltpu.SMEM((16, 128), jnp.int32),
+            pltpu.SMEM((16,), jnp.int32),
+            pltpu.VMEM((5, 128, 1024), BF16),
+            pltpu.VMEM((3, 128), BF16),
             pltpu.VMEM((2, 1024, 128), F32),
             pltpu.VMEM((2, 64, 16, 128), BF16),
             pltpu.VMEM((2, 64, 16, 128), BF16),
@@ -394,7 +437,8 @@
             pltpu.VMEM((2, 2, 4, 4, 16, 128), BF16),
             pltpu.VMEM((16, 16, 128), BF16),
             pltpu.VMEM((16, 16, 128), BF16),
-            dma,
+            pltpu.SemaphoreType.REGULAR,
+            dma((6,)),
             dma,
             dma((2, 2)),
             dma((2, 2, 2)),

time: 74.8 us -> 69.9 us (0.934)
  the two profiles are of different devices: /device:TPU:32 before, /device:TPU:1 now
where the time goes in v3:
time: 69.9 us; the launch traced here: 68.6 us
  Pallas kernels  67.3 us (96%)
  local copies, waits for them, and re-layouts  1.32 us (2%)
    pallas_call x1, Pallas kernels, local(): pl.pallas_call(kernel, out_shape=jax.ShapeDtypeStruct((32, 64), F32), in_...  67.3 us

profile of v3, /device:TPU:1, one launch (start us, length us, event | category | flops | bytes accessed | tf_op | source)
XLA Modules:
  0.0 68.6 jit_solution(7980007533364830265)
XLA Ops:
  0.0 67.3 %shard_map.64 = f32[32,64]{1,0:T(8,128)} custom-call(s32[1,1,64]{2,1,0:T(1,128)} %block_map_hbm.1, s32[16,128]{1,0:T(8,128)} %band_observers_hbm.1, s32[16]{0:T(128)} %band_lags_hbm.1, bf16[5,128,1024]{2,1,0:T(8,128)(2,1)} %surface_hbm.1, bf16[3,128]{1,0:T(4,128)(2,1)} %normals_hbm.1, bf16[6,2048,128]{2,1,0:T(8,128)(2,1)} %bitcast.1), custom_call_target="tpu_custom_call" | custom-call | tf_op jit(solution)/shard_map/pallas_call | solution.py:410
  67.3 1.3 %copy.8 = f32[32,64]{1,0:T(8,128)} copy(f32[32,64]{1,0:T(8,128)} %shard_map.64) | data formatting | bytes 16384

commit v4 on v3

--- a/solution.py
+++ b/solution.py
@@ -46,7 +46,7 @@
     recv2,
     send3,
     recv3,
-    round_sem,
+    round_sems,
     input_sems,
     table_sem,
     face_sems,
@@ -69,7 +69,7 @@
 
     barrier = pltpu.get_barrier_semaphore()
 
-    for dz in (4, -4, 3, -3, 2, -2, 1, -1, 0):
+    for dz in (2, -2, 1, -1, 0):
         there = (z + 16 + dz) % 16
         for k in range(8):
             if dz or k:
@@ -122,15 +122,18 @@
         for series in range(2):
             staging[series, d] = face_rows[series, pl.ds(first, 16), :].astype(BF16)
 
-    pl.semaphore_wait(barrier, 74)
-    for dz in (4, -4):
-        there = (z + 16 + dz) % 16
-        pl.semaphore_signal(
-            round_sem,
-            inc=1,
-            device_id=device(z_lo_=there % 8, z_hi_=there // 8),
-            device_id_type=MESH,
-        )
+    pl.semaphore_wait(barrier, 42)
+    def tell(step):
+        for dz in (2, -2):
+            there = (z + 16 + dz) % 16
+            pl.semaphore_signal(
+                round_sems.at[step],
+                inc=1,
+                device_id=device(z_lo_=there % 8, z_hi_=there // 8),
+                device_id_type=MESH,
+            )
+
+    tell(0)
 
     def send_block(series, dest_z, k):
         dest = (dest_z * 4 + (x + k // 2) % 4) * 2 + (core + k) % 2
@@ -155,11 +158,17 @@
                     for k in range(8):
                         send_block(series, dest_z, k)
 
-    send_far_to_near(0, 4, 1)
-    pl.semaphore_wait(round_sem, 2)
-    send_far_to_near(0, 7, 5)
+    send_far_to_near(0, 2, 1)
     for k in range(1, 8):
         send_block(0, z_lo, k)
+    pl.semaphore_wait(round_sems.at[0], 2)
+    tell(1)
+    send_far_to_near(0, 4, 3)
+    pl.semaphore_wait(round_sems.at[1], 2)
+    tell(2)
+    send_far_to_near(0, 6, 5)
+    pl.semaphore_wait(round_sems.at[2], 2)
+    send_far_to_near(0, 7, 7)
     send_far_to_near(1, 7, 1)
     for k in range(1, 8):
         send_block(1, z_lo, k)
@@ -373,11 +382,10 @@
             if i != 11:
                 copy3(i, False).start()
 
-    for chunk in range(2):
-        for half in (1, 0):
-            second(half, chunk)
-        for half in (1, 0):
-            third(half, chunk)
+    for stage in (second, third):
+        for chunk in range(2):
+            for half in (1, 0):
+                stage(half, chunk)
 
     total = send3[11].astype(F32)
     for i in (10, 12, 9, 13, 8, 14, 15, 7, 0, 6, 1, 5, 2, 4, 3):
@@ -437,7 +445,7 @@
             pltpu.VMEM((2, 2, 4, 4, 16, 128), BF16),
             pltpu.VMEM((16, 16, 128), BF16),
             pltpu.VMEM((16, 16, 128), BF16),
-            pltpu.SemaphoreType.REGULAR,
+            pltpu.SemaphoreType.REGULAR((3,)),
             dma((6,)),
             dma,
             dma((2, 2)),

time: 69.9 us -> 68.4 us (0.979)
  Pallas kernels: 67.3 us -> 66 us
    pallas_call x1, Pallas kernels: 67.3 us -> 66 us  [local(): pl.pallas_call(kernel, out_shape=jax.ShapeDtypeStruct((32, 64), F32), in_...]
where the time goes in v4:
time: 68.4 us; the launch traced here: 67.3 us
  Pallas kernels  66 us (96%)
  local copies, waits for them, and re-layouts  1.32 us (2%)
    pallas_call x1, Pallas kernels, local(): pl.pallas_call(kernel, out_shape=jax.ShapeDtypeStruct((32, 64), F32), in_...  66 us

profile of v4, /device:TPU:1, one launch (start us, length us, event | category | flops | bytes accessed | tf_op | source)
XLA Modules:
  0.0 67.3 jit_solution(1024068193279666649)
XLA Ops:
  0.0 66.0 %shard_map.64 = f32[32,64]{1,0:T(8,128)} custom-call(s32[1,1,64]{2,1,0:T(1,128)} %block_map_hbm.1, s32[16,128]{1,0:T(8,128)} %band_observers_hbm.1, s32[16]{0:T(128)} %band_lags_hbm.1, bf16[5,128,1024]{2,1,0:T(8,128)(2,1)} %surface_hbm.1, bf16[3,128]{1,0:T(4,128)(2,1)} %normals_hbm.1, bf16[6,2048,128]{2,1,0:T(8,128)(2,1)} %bitcast.1), custom_call_target="tpu_custom_call" | custom-call | tf_op jit(solution)/shard_map/pallas_call | solution.py:418
  66.0 1.3 %copy.8 = f32[32,64]{1,0:T(8,128)} copy(f32[32,64]{1,0:T(8,128)} %shard_map.64) | data formatting | bytes 16384

commit v5 on v4

--- a/solution.py
+++ b/solution.py
@@ -340,7 +340,7 @@
                 send1[at] = (tile + core_recv[at].astype(F32)).astype(BF16)
 
         for chunk in range(2):
-            for k in (2, 1, 3):
+            for k in (1, 3, 2):
                 copies(1, half, chunk, k, False).start()
 
     def second(half, chunk):

time: 68.4 us -> 67.5 us (0.987); the launches traced: 67.3 us -> 67.3 us
  no operation moved by 1% of the time
where the time goes in v5:
time: 67.5 us; the launch traced here: 67.3 us
  Pallas kernels  66 us (98%)
  local copies, waits for them, and re-layouts  1.32 us (2%)
    pallas_call x1, Pallas kernels, local(): pl.pallas_call(kernel, out_shape=jax.ShapeDtypeStruct((32, 64), F32), in_...  66 us

profile of v5, /device:TPU:1, one launch (start us, length us, event | category | flops | bytes accessed | tf_op | source)
XLA Modules:
  0.0 67.3 jit_solution(3705458131732824231)
XLA Ops:
  0.0 66.0 %shard_map.64 = f32[32,64]{1,0:T(8,128)} custom-call(s32[1,1,64]{2,1,0:T(1,128)} %block_map_hbm.1, s32[16,128]{1,0:T(8,128)} %band_observers_hbm.1, s32[16]{0:T(128)} %band_lags_hbm.1, bf16[5,128,1024]{2,1,0:T(8,128)(2,1)} %surface_hbm.1, bf16[3,128]{1,0:T(4,128)(2,1)} %normals_hbm.1, bf16[6,2048,128]{2,1,0:T(8,128)(2,1)} %bitcast.1), custom_call_target="tpu_custom_call" | custom-call | tf_op jit(solution)/shard_map/pallas_call | solution.py:418
  66.0 1.3 %copy.8 = f32[32,64]{1,0:T(8,128)} copy(f32[32,64]{1,0:T(8,128)} %shard_map.64) | data formatting | bytes 16384
